TPU v7x, 32 devices: a whole 2x2x4 slice. The times are simulated.
32 devices in a mesh: grp: 4 (over z), row: 8 (over y, x, core).
Axes of the slice: x: 2, y: 2, z: 4, core: 2. Of those that a mesh axis runs over, the one named last changes fastest.
Arguments:
- a_pieces: bfloat16 [4, 512, 4096], P('grp', 'row'), as said below
- touched: int32 [4, 512], P('grp', 'row'), may hold values from 0 to 7
- slot_row: int32 [512], P('row'), may hold values from 0 to 511, as said below
- x_blocks: bfloat16 [32, 64, 64], P('grp'), as said below
- z_inverse: bfloat16 [32, 64, 64], P('grp'), as said below
- block_class: int32 [32], P('grp'), may hold values from 0 to 1
Outputs:
- schur: float32 [512, 512], P('row', 'grp')
Inputs may be any that keep to these rules, and one draw needn't show every extreme that they name: `slot_row`: A permutation of the constraints. The 64 slots of one index r of row (slots r * 64 onward) hold, of the constraints o * 64 to (o + 1) * 64 - 1 of each index o, either none or exactly 16. `a_pieces`: each piece read as a 64 x 64 matrix is symmetric. `x_blocks`: each block is symmetric positive definite. `z_inverse`: each block is symmetric positive definite.
All inputs are finite; a program needn't handle non-finite values.
Results may differ from a plain program's by a relative error of at most 0.0008.
Values may be sent and summed in bfloat16 or wider, within the bound.
A program may use at most 64 MiB of HBM per device.

v0:
```python
import jax
import jax.numpy as jnp
from jax import lax
from jax.sharding import PartitionSpec as P


def masked_blocks(blocks, block_class):
    block_order = blocks.shape[1]
    positions = jnp.arange(block_order)
    active = block_order // 2 * (1 + block_class)
    inside = (positions[None, :, None] < active[:, None, None]) & (
        positions[None, None, :] < active[:, None, None]
    )
    return jnp.where(inside, blocks, jnp.zeros_like(blocks))


def shards(a_pieces, touched, slot_row, x_blocks, z_inverse, block_class):
    local_rows = a_pieces.shape[1]
    block_order = x_blocks.shape[1]
    flat_len = a_pieces.shape[2]
    x_masked = masked_blocks(x_blocks, block_class)
    z_masked = masked_blocks(z_inverse, block_class)
    own_block = touched[0]
    a_local = a_pieces[0]
    pieces = a_local.reshape(local_rows, block_order, block_order)
    left_part = jnp.einsum(
        "rab,rbc->rac", x_masked[own_block], pieces, preferred_element_type=jnp.float32
    ).astype(jnp.bfloat16)
    product = jnp.einsum(
        "rab,rbc->rac", left_part, z_masked[own_block], preferred_element_type=jnp.float32
    ).astype(jnp.bfloat16)
    product_flat = product.reshape(local_rows, flat_len)
    all_slots, all_kinds = (
        lax.all_gather(slot_row, "row", axis=0, tiled=True),
        lax.all_gather(touched, "row", axis=1, tiled=True),
    )
    constraints = all_slots.shape[0]
    kinds_flat = all_kinds[0]
    scores = lax.dot_general(
        product_flat,
        lax.all_gather(a_local, "row", axis=0, tiled=True),
        (((1,), (1,)), ((), ())),
        preferred_element_type=jnp.float32,
    )
    scores = jnp.where(own_block[:, None] == kinds_flat[None, :], scores, jnp.zeros_like(scores))
    inverse = (
        jnp.zeros((constraints,), jnp.int32)
        .at[all_slots]
        .set(jnp.arange(constraints, dtype=jnp.int32))
    )
    ordered = scores[:, inverse]
    summed = lax.psum_scatter(ordered, "grp", scatter_dimension=1, tiled=True)
    columns = summed.shape[1]
    devices = lax.axis_size("row")
    slot_cap = max(2, local_rows // devices * 2)
    owners = slot_row // local_rows
    earlier = jnp.arange(local_rows)[None, :] < jnp.arange(local_rows)[:, None]
    rank_send = jnp.sum(((owners[:, None] == owners[None, :]) & earlier).astype(jnp.int32), axis=1)
    send_slot = owners * slot_cap + rank_send
    outgoing = jnp.zeros((devices * slot_cap, columns), jnp.float32).at[send_slot].set(summed)
    incoming = lax.all_to_all(outgoing, "row", split_axis=0, concat_axis=0, tiled=True)
    my_row = lax.axis_index("row")
    table_ids = all_slots.reshape(devices, local_rows)
    arrives = table_ids // local_rows == my_row
    rank_recv = jnp.cumsum(arrives.astype(jnp.int32), axis=1) - 1
    source_base = (jnp.arange(devices, dtype=jnp.int32) * slot_cap)[:, None]
    target = jnp.where(arrives, source_base + rank_recv, devices * slot_cap)
    landing = jnp.full((devices * slot_cap + 1,), local_rows, jnp.int32)
    landing = landing.at[target.reshape(-1)].set((table_ids % local_rows).reshape(-1))
    result = (
        jnp.zeros((local_rows, columns), jnp.float32).at[landing[:-1]].set(incoming, mode="drop")
    )
    return result


def solution(mesh):
    return jax.shard_map(
        shards,
        mesh=mesh,
        in_specs=(
            P("grp", "row", None),
            P("grp", "row"),
            P("row"),
            P("grp", None, None),
            P("grp", None, None),
            P("grp"),
        ),
        out_specs=P("row", "grp"),
        check_vma=False,
    )
```

profile of v0, /device:TPU:0, one launch (start us, length us, event | category | flops | bytes accessed | tf_op | source)
XLA Modules:
  0.0 93.4 jit_solution(4507066098227181438)
XLA Ops:
  6.5 0.0 all-gather.3.cloned.1.call-start
  6.5 0.7 all-gather.3.cloned.1.call-update
  7.3 0.0 reduce-scatter.2.cloned.1.call-start
  7.3 2.1 %reshape_squeeze.3 = bf16[64,64,64]{2,1,0:T(8,128)(2,1)S(1)} reshape(bf16[1,64,4096]{2,1,0:T(8,128)(2,1)} %param.6) | data formatting | bytes 1048576 | tf_op jit(solution)/shard_map/reshape;squeeze | solution.py:25
  9.4 1.2 %dynamic-slice = u32[1]{0:T(128)} dynamic-slice(u32[32]{0:T(128)} %constant.77, u32[]{:T(128)S(6)} %add.84), dynamic_slice_sizes={1} | dynamic-slice | bytes 12
  11.3 0.9 dynamic-update-slice
  12.1 0.7 bitcast_dynamic-update-slice_fusion
  12.9 9.5 %all-reduce.2 = (s32[512]{0:T(512)S(1)}, s32[512]{0:T(512)S(1)}) all-reduce(s32[512]{0:T(512)S(1)} %dynamic-update-slice, s32[512]{0:T(512)S(1)} %bitcast_dynamic-update-slice_fusion), channel_id=1, replica_groups=mesh['grp'=4,'row'=8] {'row'}, use_global_device_ids=true, to_apply=%add | all-reduce | flops 1024 | bytes 8192
  22.4 0.1 reshape.95
  22.5 0.2 reduce_window_sum.11
  22.7 0.1 add_add_fusion
  22.8 0.1 add.71
  22.8 0.7 fusion.18
  23.5 0.7 add_multiply_fusion
  24.2 0.1 iota_compare_fusion.1
  24.2 1.1 %and_select_fusion.1 = (bf16[8,64,64]{2,1,0:T(8,128)(2,1)S(1)}, bf16[8,64,64]{2,1,0:T(8,128)(2,1)S(1)}) fusion(bf16[8,64,64]{2,1,0:T(8,128)(2,1)} %param.9, pred[8,64]{1,0:T(8,128)(4,1)S(1)} %iota_compare_fusion.1, bf16[8,64,64]{2,1,0:T(8,128)(2,1)} %param.10), kind=kLoop, calls=%fused_computation.13 | loop fusion | flops 98304 | bytes 262656 | tf_op jit(solution)/shard_map/jit(_where)/select_n | solution.py:14
  25.4 0.7 gather_fusion.1
  26.1 0.0 copy-start.1
  26.1 0.0 copy-start
  26.1 0.7 gather_fusion
  26.9 1.7 %convolution_convert_fusion = bf16[64,64,64]{2,1,0:T(8,128)(2,1)} fusion(bf16[64,64,64]{2,1,0:T(8,128)(2,1)S(1)} %gather_fusion.1, bf16[64,64,64]{2,1,0:T(8,128)(2,1)S(1)} %gather_fusion, bf16[64,64,64]{2,1,0:T(8,128)(2,1)S(1)} %reshape_squeeze.3), kind=kOutput, calls=%fused_computation.9 | convolution fusion | flops 67633152 | bytes 2097152 | tf_op jit(solution)/shard_map/rab,rbc->rac/dot_general | solution.py:29
  28.6 2.1 %reshape.96 = bf16[64,4096]{1,0:T(8,128)(2,1)S(1)} reshape(bf16[64,64,64]{2,1,0:T(8,128)(2,1)} %convolution_convert_fusion) | data formatting | bytes 1048576 | tf_op jit(solution)/shard_map/reshape | solution.py:32
  30.7 2.4 %scatter_custom_fusion.1 = s32[512]{0:T(512)S(1)} fusion(s32[512]{0:T(512)S(1)} %get-tuple-element.7, s32[512]{0:T(512)S(1)} %iota.33, s32[]{:T(128)} %constant.35.clone.1), kind=kCustom, calls=%fused_computation.52 | custom fusion | bytes 2052 | tf_op jit(solution)/shard_map/scatter | solution.py:49
  33.2 0.0 copy-done.1
  33.2 15.4 %all-gather.3.cloned.1.call-done = bf16[1,512,4096]{2,1,0:T(8,128)(2,1)} async-done(((bf16[1,64,4096]{2,1,0:T(8,128)(2,1)}), bf16[1,512,4096]{2,1,0:T(8,128)(2,1)}) %all-gather.3.cloned.1.call-update) | async-done | bytes 4194320 | tf_op jit(solution)/shard_map/all_gather | solution.py:41
  48.6 0.0 copy-done
  48.6 3.6 %fusion.2 = f32[64,512]{1,0:T(8,128)S(1)} fusion(bf16[64,4096]{1,0:T(8,128)(2,1)S(1)} %reshape.96, bf16[1,512,4096]{2,1,0:T(8,128)(2,1)} %all-gather.3.cloned.1.call-done, s32[512]{0:T(512)S(1)} %get-tuple-element.6, s32[64]{0:T(128)S(1)} %bitcast.21), kind=kOutput, calls=%fused_computation.11 | convolution fusion | flops 268500992 | bytes 4851968 | tf_op jit(solution)/shard_map/dot_general | solution.py:39
  52.2 0.1 copy.10
  52.3 1.6 %gather_fusion.2 = f32[512,64]{1,0:T(8,128)} fusion(f32[64,512]{0,1:T(8,128)S(1)} %copy.10, s32[1024]{0:T(1024)S(1)} %pad_clamp_fusion), kind=kCustom, calls=%fused_computation.2 | custom fusion | bytes 264192 | tf_op jit(solution)/shard_map/gather | solution.py:51
  54.0 0.0 reduce-scatter.2.cloned.1.call-update
  54.0 0.2 convert_reduce_fusion
  54.2 2.4 %scatter_custom_fusion = s32[129]{0:T(256)S(1)} fusion(s32[512]{0:T(512)S(1)} %get-tuple-element.9, s32[512]{0:T(512)S(1)} %get-tuple-element.8, s32[]{:T(128)} %constant.33.clone.1), kind=kCustom, calls=%fused_computation.58 | custom fusion | bytes 520 | tf_op jit(solution)/shard_map/scatter | solution.py:69
  56.6 17.5 %reduce-scatter.2.cloned.1.call-done = f32[64,128]{0,1:T(8,128)} async-done(((f32[64,512]{0,1:T(8,128)}), f32[64,128]{0,1:T(8,128)}) %reduce-scatter.2.cloned.1.call-update) | async-done | bytes 32784 | tf_op jit(solution)/shard_map/reduce_scatter | solution.py:52
  74.1 0.9 copy.11
  75.0 1.3 %scatter_custom_fusion.2 = f32[128,128]{1,0:T(8,128)} fusion(s32[64]{0:T(128)S(1)} %compare_select_fusion.3, f32[64,128]{1,0:T(8,128)S(1)} %copy.11, f32[]{:T(128)} %constant.31.clone.1), kind=kCustom, calls=%fused_computation.16 | custom fusion | bytes 65540 | tf_op jit(solution)/shard_map/scatter | solution.py:60
  76.4 3.7 %all-to-all-start = ((f32[8,16,128]{2,1,0:T(8,128)}), f32[8,16,128]{2,1,0:T(8,128)S(1)}, u32[]{:S(2)}, u32[]{:S(2)}) async-start(f32[8,16,128]{2,1,0:T(8,128)} %bitcast.6), calls=%async_computation.1 | async-start | bytes 131072 | tf_op jit(solution)/shard_map/all_to_all | solution.py:61
  80.1 5.0 %all-to-all-done = f32[8,16,128]{2,1,0:T(8,128)S(1)} async-done(((f32[8,16,128]{2,1,0:T(8,128)}), f32[8,16,128]{2,1,0:T(8,128)S(1)}, u32[]{:S(2)}, u32[]{:S(2)}) %all-to-all-start) | async-done | bytes 65568 | tf_op jit(solution)/shard_map/all_to_all | solution.py:61
  85.1 1.4 %scatter_custom_fusion.3 = f32[64,128]{1,0:T(8,128)} fusion(s32[128]{0:T(128)S(1)} %compare_select_fusion.4, f32[128,128]{1,0:T(8,128)S(1)} %bitcast.20, f32[]{:T(128)} %constant.31.clone.1), kind=kCustom, calls=%fused_computation.19 | custom fusion | bytes 32772 | tf_op jit(solution)/shard_map/scatter | solution.py:71
  (12 shorter events, 0.1 us)
Async XLA Ops:
  6.5 42.1 %all-gather.3.cloned.1.call-start = ((), (), s32[]{:S(2)}) async-start(), calls=%async_computation.3 | async-start | bytes 4718592 | tf_op jit(solution)/shard_map/all_gather | solution.py:41
  7.3 66.9 %reduce-scatter.2.cloned.1.call-start = ((), (), s32[]{:S(2)}) async-start(), calls=%async_computation.2 | async-start | bytes 327680 | tf_op jit(solution)/shard_map/reduce_scatter | solution.py:52
  26.1 7.0 %copy-start.1 = (s32[64]{0:T(128)S(1)}, s32[64]{0:T(128)}, u32[]{:S(2)}) copy-start(s32[64]{0:T(128)} %param.8) | copy-start | bytes 772
  26.1 22.5 %copy-start = (s32[1,64]{1,0:T(1,128)S(1)}, s32[1,64]{1,0:T(1,128)}, u32[]{:S(2)}) copy-start(s32[1,64]{1,0:T(1,128)} %param.7) | copy-start | bytes 772
  76.4 8.7 %all-to-all-start = ((f32[8,16,128]{2,1,0:T(8,128)}), f32[8,16,128]{2,1,0:T(8,128)S(1)}, u32[]{:S(2)}, u32[]{:S(2)}) async-start(f32[8,16,128]{2,1,0:T(8,128)} %bitcast.6), calls=%async_computation.1 | async-start | bytes 131072 | tf_op jit(solution)/shard_map/all_to_all | solution.py:61
Sparse Core Ops, SparseCore 0:
  9.2 39.3 all-gather.2
  54.1 19.9 reduce-scatter.1
where the time goes:
time: 93.7 us; the launch traced here: 93.4 us
  waiting for transfers between devices  38.7 us (41%)
  local copies, waits for them, and re-layouts  19 us (20%)
  between operations  14.2 us (15%)
  blocking collectives  9.49 us (10%)
  matrix products  5.27 us (6%)
  starting transfers between devices  3.72 us (4%)
  other arithmetic  3.04 us (3%)
    reduce_scatter x1, waiting for transfers between devices, shards(): summed = lax.psum_scatter(ordered, 'grp', scatter_dimension=1, tiled=True)  17.5 us
    all_gather x1, waiting for transfers between devices, shards(): lax.all_gather(a_local, 'row', axis=0, tiled=True)  15.4 us
    unnamed x1, blocking collectives  9.49 us
    all_to_all x1, waiting for transfers between devices, shards(): lax.all_to_all(outgoing, 'row', split_axis=0, concat_axis=0, tiled=True)  5.01 us
    all_to_all x1, starting transfers between devices, shards(): lax.all_to_all(outgoing, 'row', split_axis=0, concat_axis=0, tiled=True)  3.68 us
    dot_general x1, matrix products, shards(): lax.dot_general(product_flat, lax.all_gather(a_local, 'row', axis=0, tile...  3.58 us
    unnamed x9, local copies, waits for them, and re-layouts  2.86 us
    scatter x1, local copies, waits for them, and re-layouts, shards(): landing.at[target.reshape(-1)].set((table_ids % local_rows).reshape(-1))  2.44 us
  transfers between devices with their start and end apart: 3, of which 3 were waited for; matrix products, arithmetic and copies ran while one was open for 20% of the time, Pallas kernels for 0%

commit v1 on v0

v1 whole, which is shorter than its diff:
```python
import functools
import jax
import jax.numpy as jnp
from jax import lax
from jax.experimental import pallas as pl
from jax.experimental.pallas import tpu as pltpu
from jax.sharding import PartitionSpec as P

F32, BF16, I32 = jnp.float32, jnp.bfloat16, jnp.int32
LANES = 128


def iota(shape, dim):
    return lax.broadcasted_iota(I32, shape, dim)


def mm(a, b):
    return lax.dot_general(a, b, (((1,), (0,)), ((), ())), preferred_element_type=F32)


def mm_nt(a, b):
    return lax.dot_general(a, b, (((1,), (1,)), ((), ())), preferred_element_type=F32)


def split(v):
    hi = v.astype(BF16)
    return hi, (v - hi.astype(F32)).astype(BF16)


def onehot(mask):
    return jnp.where(mask, 1.0, 0.0).astype(BF16)


def kernel(
    n, ng, cap,
    a_ref, touched_s, class_s, touched_v, slot_v, x_ref, z_ref,
    out_ref,
    gath, meta, w_ref, zm_ref, l3, p3, q_ref, score, zsend, zrecv, osend, orecv,
    g_send, g_recv, m_send, m_recv, z_ssem, z_rsem, o_send, o_recv,
):
    rows, flat = a_ref.shape[1], a_ref.shape[2]
    kinds, nb = x_ref.shape[0], x_ref.shape[1]
    half = nb // 2
    tiles = flat // LANES
    fold = tiles // 2
    hrows = rows // 2
    pairs = n // 2
    cols = out_ref.shape[1]
    g, me = lax.axis_index("grp"), lax.axis_index("row")

    def rdma(src, dst, ssem, rsem, dev):
        return pltpu.make_async_remote_copy(
            src_ref=src, dst_ref=dst, send_sem=ssem, recv_sem=rsem,
            device_id=dev, device_id_type=pl.DeviceIdType.MESH,
        )

    def row_peer(d):
        return lax.rem(me + d, n)

    def grp_peer(d):
        return lax.rem(g + d, ng)

    barrier = pltpu.get_barrier_semaphore()
    for d in range(1, n):
        pl.semaphore_signal(
            barrier, inc=1, device_id=(g, row_peer(d)), device_id_type=pl.DeviceIdType.MESH
        )
    for d in range(1, ng):
        pl.semaphore_signal(
            barrier, inc=1, device_id=(grp_peer(d), me), device_id_type=pl.DeviceIdType.MESH
        )

    lane = iota((rows, LANES), 1)
    in_row = lax.rem(lane, nb)
    second = (lane >= nb).astype(I32)

    def pack(top, bottom, t):
        turned = pltpu.roll(bottom, LANES - half, 1)
        return jnp.where(in_row < 2 * t + second, turned, top)

    def diagonal(bottom, t):
        hit = in_row == half + 2 * t + second
        return jnp.where(hit, bottom, 0.0)

    extra = jnp.zeros((rows, LANES), F32)
    for t in range(fold):
        top = a_ref[0, :, t * LANES:(t + 1) * LANES].astype(F32)
        bottom = a_ref[0, :, (t + fold) * LANES:(t + fold + 1) * LANES].astype(F32)
        gath[me, :, t * LANES:(t + 1) * LANES] = pack(top, bottom, t).astype(BF16)
        extra = extra + diagonal(bottom, t)
    gath[me, :, fold * LANES:(fold + 1) * LANES] = extra.astype(BF16)

    core = lax.rem(me, 2)
    meta[me] = jnp.full((8, LANES), -1, I32)
    meta[me, 0:1, 0:rows] = touched_v[...]
    meta[me, 1:2, 0:rows] = slot_v[...]
    own_meta = meta[me]
    own_touched = own_meta[0:1, :]
    own_slot = own_meta[1:2, :]
    meta[me] = jnp.where(core == 1, pltpu.roll(own_meta, rows, 1), own_meta)

    pl.semaphore_wait(barrier, n - 1 + ng - 1)

    started = []

    def go(src, dst, ssem, rsem, dev):
        c = rdma(src, dst, ssem, rsem, dev)
        c.start()
        started.append(c)

    counter = [0]

    def send_half(s, h, dst_row):
        k = counter[0]
        counter[0] += 1
        view = gath.at[s, pl.ds(h * hrows, hrows)]
        go(view, view, g_send.at[k], g_recv.at[s, h], (g, dst_row))

    def wait_half(s, h):
        view = gath.at[s, pl.ds(h * hrows, hrows)]
        rdma(view, view, g_send.at[0], g_recv.at[s, h], (g, row_peer(1))).wait_recv()

    relay = n == 8
    if relay:
        def flip(v, bit):
            return v + bit - 2 * bit * lax.rem(lax.div(v, bit), 2)
        sib, xn, yn = flip(me, 1), flip(me, 2), flip(me, 4)
        dn = flip(xn, 4)
        send_half(me, 0, xn)
        send_half(me, 1, yn)
        send_half(me, 1, xn)
        send_half(me, 0, yn)
        send_half(me, 0, sib)
        send_half(me, 1, sib)
    else:
        for d in range(1, n):
            for h in range(2):
                send_half(me, h, row_peer(d))
    for d in range(1, n):
        go(meta.at[me], meta.at[me], m_send.at[d], m_recv.at[me], (g, row_peer(d)))

    r64, c64 = iota((nb, nb), 0), iota((nb, nb), 1)
    dup = onehot(lax.rem(iota((nb, LANES), 1), nb) == iota((nb, LANES), 0))
    lane_b = iota((nb, LANES), 1)
    for k in range(kinds):
        active = half * (1 + class_s[k])
        inside = (r64 < active) & (c64 < active)
        xm = jnp.where(inside, x_ref[k].astype(F32), 0.0).astype(BF16)
        zm_ref[k] = jnp.where(inside, z_ref[k].astype(F32), 0.0).astype(BF16)
        wide = mm(xm, dup)
        w_ref[0:nb, k * LANES:(k + 1) * LANES] = jnp.where(lane_b < nb, wide, 0.0).astype(BF16)
        w_ref[nb:2 * nb, k * LANES:(k + 1) * LANES] = jnp.where(lane_b >= nb, wide, 0.0).astype(BF16)

    spread = jnp.broadcast_to(own_touched, (LANES, LANES)).astype(F32)
    own_kind = jnp.transpose(spread)[0:rows, :]

    def left_tile(t, carry):
        off = pl.multiple_of(t * LANES, LANES)
        at = a_ref[0, :, pl.ds(off, LANES)]
        full = mm(at, w_ref[...])
        acc = jnp.zeros((rows, LANES), F32)
        for k in range(kinds):
            acc = acc + jnp.where(own_kind == k, full[:, k * LANES:(k + 1) * LANES], 0.0)
        acc = acc.astype(BF16).astype(F32)
        l3[pl.ds(2 * t, rows, stride=nb), :] = acc
        l3[pl.ds(2 * t + 1, rows, stride=nb), :] = pltpu.roll(acc, nb, 1)
        return carry

    def left_tiles(u, carry):
        for v in range(4):
            left_tile(u * 4 + v, carry)
        return carry

    lax.fori_loop(0, tiles // 4, left_tiles, 0)

    eye = onehot(r64 == c64)

    def product_step(u, carry):
        for v in range(8):
            i = u * 8 + v
            off = pl.multiple_of(i * nb, nb)
            lt = l3[pl.ds(off, nb), 0:nb].astype(BF16)
            zk = zm_ref[touched_s[0, i]]
            pt = mm(zk, lt).astype(BF16)
            ptf = pt.astype(F32)
            p3[pl.ds(off, nb), 0:nb] = jnp.where(r64 == c64, ptf, ptf + mm_nt(eye, pt))
        return carry

    steps = rows // 8
    if relay:
        lax.fori_loop(0, steps // 2, product_step, 0)
        wait_half(xn, 0)
        send_half(xn, 0, yn)
        send_half(xn, 0, sib)
        wait_half(yn, 1)
        send_half(yn, 1, xn)
        send_half(yn, 1, sib)
        lax.fori_loop(steps // 2, steps, product_step, 0)
        wait_half(xn, 1)
        send_half(xn, 1, sib)
        wait_half(yn, 0)
        send_half(yn, 0, sib)
    else:
        lax.fori_loop(0, steps, product_step, 0)

    low_lane = lane < nb
    qextra = jnp.zeros((rows, LANES), F32)

    def put(t, v):
        hi, lo = split(v)
        q_ref[0:rows, t * LANES:(t + 1) * LANES] = hi
        q_ref[rows:2 * rows, t * LANES:(t + 1) * LANES] = lo

    def flat_tile(t):
        even = p3[pl.ds(2 * t, rows, stride=nb), :]
        odd = p3[pl.ds(2 * t + 1, rows, stride=nb), :]
        return jnp.where(low_lane, even, pltpu.roll(odd, nb, 1))

    for t in range(fold):
        top, bottom = flat_tile(t), flat_tile(t + fold)
        put(t, pack(top, bottom, t))
        qextra = qextra + diagonal(bottom, t)
    put(fold, qextra)

    for d in range(1, n):
        s = row_peer(d)
        rdma(meta.at[s], meta.at[s], m_send.at[d], m_recv.at[s], (g, s)).wait_recv()

    def pair_meta(p):
        return jnp.maximum(meta[2 * p], meta[2 * p + 1])

    def score_pair(p):
        block = gath[pl.ds(2 * p, 2)].reshape(2 * rows, gath.shape[2])
        s = mm_nt(q_ref[...], block)
        s = s[0:rows] + s[rows:2 * rows]
        kind = pair_meta(p)[0:1, :].astype(F32)
        score[p] = jnp.where(own_kind == kind, s, 0.0)

    mine = lax.div(me, 2)
    if relay:
        wait_half(sib, 0)
        wait_half(sib, 1)
        score_pair(mine)
        sx, sy, sd = flip(sib, 2), flip(sib, 4), flip(flip(sib, 2), 4)
        wait_half(sx, 0)
        wait_half(sx, 1)
        score_pair(lax.div(xn, 2))
        wait_half(dn, 0)
        send_half(dn, 0, sib)
        wait_half(dn, 1)
        send_half(dn, 1, sib)
        wait_half(sy, 0)
        wait_half(sy, 1)
        score_pair(lax.div(yn, 2))
        wait_half(sd, 0)
        wait_half(sd, 1)
        score_pair(lax.div(dn, 2))
    else:
        for d in range(1, n):
            for h in range(2):
                wait_half(row_peer(d), h)

        def each(p, carry):
            score_pair(p)
            return carry

        lax.fori_loop(0, pairs, each, 0)

    def column_slice(q):
        def body(p, acc):
            want = q * cols + iota((cols, LANES), 0)
            table = onehot(pair_meta(p)[1:2, :] == want)
            hi, lo = split(score[p])
            both = mm_nt(jnp.concatenate([hi, lo], axis=0), table)
            return acc + both[0:rows] + both[rows:2 * rows]
        acc = jnp.zeros((rows, cols), F32)
        if pairs <= 4:
            for p in range(pairs):
                acc = body(p, acc)
            return acc
        return lax.fori_loop(0, pairs, body, acc)

    for d in range(1, ng):
        q = grp_peer(d)
        zsend[d] = column_slice(q)
        go(zsend.at[d], zrecv.at[g], z_ssem.at[d], z_rsem.at[g], (q, me))
    total = column_slice(g)

    i0, i1 = iota((LANES, LANES), 0), iota((LANES, LANES), 1)
    before = onehot((i0 < i1) & ((i0 < rows) == (i1 < rows)))
    o_id = iota((n, LANES), 0)
    owner = (own_slot >= o_id * rows) & (own_slot < (o_id + 1) * rows)
    owner_f = jnp.where(owner, 1.0, 0.0)
    rank = mm(onehot(owner), before)
    place = jnp.where(owner, rank + (o_id * cap).astype(F32) + 1.0, 0.0)
    place = jnp.sum(place, axis=0, keepdims=True).astype(I32) - 1
    route = onehot(iota((n * cap, LANES), 0) == place)[:, 0:rows]

    def landing(p):
        slots = pair_meta(p)[1:2, :]
        arrives = (slots >= me * rows) & (slots < (me + 1) * rows)
        arr = jnp.broadcast_to(jnp.where(arrives, 1.0, 0.0), (8, LANES)).astype(BF16)
        rank_in = mm(arr, before)[0:1, :].astype(I32)
        upper = (iota((1, LANES), 1) >= rows).astype(I32)
        at = jnp.where(arrives, rank_in + upper * cap, -1)
        pick = onehot(iota((2 * cap, LANES), 0) == at)
        where_to = onehot(slots == me * rows + iota((rows, LANES), 0))
        return mm_nt(where_to, pick).astype(BF16)

    lands = [landing(p) for p in range(pairs)]

    for d in range(1, ng):
        s = grp_peer(d)
        rdma(zsend.at[d], zrecv.at[s], z_ssem.at[d], z_rsem.at[s], (s, me)).wait_recv()
        total = total + zrecv[s]

    hi, lo = split(total)
    osend[...] = (mm(route, hi) + mm(route, lo)).reshape(osend.shape)
    for d in range(1, n):
        o = row_peer(d)
        go(osend.at[o], orecv.at[me], o_send.at[d], o_recv.at[me], (g, o))
    orecv[me] = osend[me]
    for d in range(1, n):
        s = row_peer(d)
        rdma(osend.at[s], orecv.at[s], o_send.at[d], o_recv.at[s], (g, s)).wait_recv()
    result = jnp.zeros((rows, cols), F32)
    for p in range(pairs):
        hi, lo = split(orecv[2 * p:2 * p + 2].reshape(2 * cap, cols))
        result = result + mm(lands[p], hi) + mm(lands[p], lo)
    out_ref[...] = result
    for c in started:
        c.wait_send()


def shards(n, ng, a_pieces, touched, slot_row, x_blocks, z_inverse, block_class):
    rows, flat = a_pieces.shape[1], a_pieces.shape[2]
    kinds, nb = x_blocks.shape[0], x_blocks.shape[1]
    packed = (flat // LANES // 2 + 1) * LANES
    cols = rows * n // ng
    cap = -(-max(2, rows // n * 2) // 8) * 8
    sends = 14 if n == 8 else 2 * n
    vmem = pl.BlockSpec(memory_space=pltpu.VMEM)
    smem = pl.BlockSpec(memory_space=pltpu.SMEM)
    dma = pltpu.SemaphoreType.DMA
    return pl.pallas_call(
        functools.partial(kernel, n, ng, cap),
        out_shape=jax.ShapeDtypeStruct((rows, cols), F32),
        in_specs=[vmem, smem, smem, vmem, vmem, vmem, vmem],
        out_specs=vmem,
        scratch_shapes=[
            pltpu.VMEM((n, rows, packed), BF16),
            pltpu.VMEM((n, 8, LANES), I32),
            pltpu.VMEM((2 * nb, kinds * LANES), BF16),
            pltpu.VMEM((kinds, nb, nb), BF16),
            pltpu.VMEM((rows * nb, LANES), F32),
            pltpu.VMEM((rows * nb, LANES), F32),
            pltpu.VMEM((2 * rows, packed), BF16),
            pltpu.VMEM((n // 2, rows, LANES), F32),
            pltpu.VMEM((ng, rows, cols), F32),
            pltpu.VMEM((ng, rows, cols), F32),
            pltpu.VMEM((n, cap, cols), F32),
            pltpu.VMEM((n, cap, cols), F32),
            dma((sends,)), dma((n, 2)), dma((n,)), dma((n,)),
            dma((ng,)), dma((ng,)), dma((n,)), dma((n,)),
        ],
        compiler_params=pltpu.CompilerParams(
            collective_id=0, has_side_effects=True, vmem_limit_bytes=56 * 1024 * 1024
        ),
    )(a_pieces, touched, block_class, touched, slot_row.reshape(1, rows), x_blocks, z_inverse)


def solution(mesh):
    n, ng = mesh.shape["row"], mesh.shape["grp"]
    return jax.shard_map(
        functools.partial(shards, n, ng),
        mesh=mesh,
        in_specs=(
            P("grp", "row", None),
            P("grp", "row"),
            P("row"),
            P("grp", None, None),
            P("grp", None, None),
            P("grp"),
        ),
        out_specs=P("row", "grp"),
        check_vma=False,
    )
```

time: 93.7 us -> 31.5 us (0.34)
  waiting for transfers between devices: 38.7 us -> 0 us
  Pallas kernels: 0 us -> 29.9 us
  local copies, waits for them, and re-layouts: 19 us -> 1.38 us
  between operations: 14.2 us -> 0.01 us
  blocking collectives: 9.49 us -> 0 us
  matrix products: 5.27 us -> 0 us
  starting transfers between devices: 3.72 us -> 0 us
  other arithmetic: 3.04 us -> 0 us
    pallas_call x0 -> x1, Pallas kernels: none -> 29.9 us  [shards(): pl.pallas_call(functools.partial(kernel, n, ng, cap), out_shape=jax.Shape...]
    reduce_scatter x1 -> x0, waiting for transfers between devices: 17.5 us -> none  [shards(): summed = lax.psum_scatter(ordered, 'grp', scatter_dimension=1, tiled=True)]
    all_gather x1 -> x0, waiting for transfers between devices: 15.4 us -> none  [shards(): lax.all_gather(a_local, 'row', axis=0, tiled=True)]
    unnamed x1 -> x0, blocking collectives: 9.49 us -> none
    scatter x4 -> x0, local copies, waits for them, and re-layouts: 7.65 us -> none  [the longest x1 2.44 us: shards(): landing.at[target.reshape(-1)].set((table_ids % local_rows).reshape(-1))]
    dot_general x2 -> x0, matrix products: 5.27 us -> none  [the longest x1 3.58 us: shards(): lax.dot_general(product_flat, lax.all_gather(a_local, 'row', axis=0, tile...]
    all_to_all x1 -> x0, waiting for transfers between devices: 5.01 us -> none  [shards(): lax.all_to_all(outgoing, 'row', split_axis=0, concat_axis=0, tiled=True)]
    all_to_all x1 -> x0, starting transfers between devices: 3.68 us -> none  [shards(): lax.all_to_all(outgoing, 'row', split_axis=0, concat_axis=0, tiled=True)]
  transfers between devices with their start and end apart: 3 -> 0, of which waited for: 3 -> 0; matrix products, arithmetic and copies ran while one was open for 20% -> 0% of each run, Pallas kernels for 0% -> 0%
where the time goes in v1:
time: 31.5 us; the launch traced here: 31.3 us
  Pallas kernels  29.9 us (95%)
  local copies, waits for them, and re-layouts  1.38 us (4%)
    pallas_call x1, Pallas kernels, shards(): pl.pallas_call(functools.partial(kernel, n, ng, cap), out_shape=jax.Shape...  29.9 us
    unnamed x1, local copies, waits for them, and re-layouts  1.38 us

profile of v1, /device:TPU:0, one launch (start us, length us, event | category | flops | bytes accessed | tf_op | source)
XLA Modules:
  0.0 31.3 jit_solution(18300270873880753557)
XLA Ops:
  0.0 29.9 %shard_map.64 = f32[64,128]{1,0:T(8,128)} custom-call(bf16[1,64,4096]{2,1,0:T(8,128)(2,1)} %a_ref.1, s32[1,64]{1,0:T(1,128)} %touched_v.1, s32[8]{0:T(128)} %class_s.1, s32[1,64]{1,0:T(1,128)} %touched_v.1, s32[1,64]{1,0:T(1,128)} %bitcast.1, bf16[8,64,64]{2,1,0:T(8,128)(2,1)} %x_ref.1, bf16[8,64,64]{2,1,0:T(8,128)(2,1)} %z_ref.1), custom_call_target="tpu_custom_call" | custom-call | tf_op jit(solution)/shard_map/pallas_call | solution.py:345
  29.9 1.4 %copy.8 = f32[64,128]{1,0:T(8,128)} copy(f32[64,128]{1,0:T(8,128)} %shard_map.64) | data formatting | bytes 65536

commit v2 on v1

--- a/solution.py
+++ b/solution.py
@@ -33,8 +33,9 @@
 
 def kernel(
     n, ng, cap,
-    a_ref, touched_s, class_s, touched_v, slot_v, x_ref, z_ref,
+    a_hbm, touched_hbm, class_s, slot_hbm, x_hbm, z_hbm,
     out_ref,
+    a_ref, touched_s, touched_v, slot_v, x_ref, z_ref, in_sem,
     gath, meta, w_ref, zm_ref, l3, p3, q_ref, score, zsend, zrecv, osend, orecv,
     g_send, g_recv, m_send, m_recv, z_ssem, z_rsem, o_send, o_recv,
 ):
@@ -45,7 +46,7 @@
     fold = tiles // 2
     hrows = rows // 2
     pairs = n // 2
-    cols = out_ref.shape[1]
+    cols = out_ref.shape[2]
     g, me = lax.axis_index("grp"), lax.axis_index("row")
 
     def rdma(src, dst, ssem, rsem, dev):
@@ -70,6 +71,16 @@
             barrier, inc=1, device_id=(grp_peer(d), me), device_id_type=pl.DeviceIdType.MESH
         )
 
+    loads = [
+        pltpu.make_async_copy(src, dst, in_sem.at[k])
+        for k, (src, dst) in enumerate((
+            (a_hbm, a_ref), (touched_hbm, touched_v), (slot_hbm, slot_v),
+            (touched_hbm, touched_s), (x_hbm, x_ref), (z_hbm, z_ref),
+        ))
+    ]
+    for c in loads:
+        c.start()
+
     lane = iota((rows, LANES), 1)
     in_row = lax.rem(lane, nb)
     second = (lane >= nb).astype(I32)
@@ -82,6 +93,8 @@
         hit = in_row == half + 2 * t + second
         return jnp.where(hit, bottom, 0.0)
 
+    for c in loads[:3]:
+        c.wait()
     extra = jnp.zeros((rows, LANES), F32)
     for t in range(fold):
         top = a_ref[0, :, t * LANES:(t + 1) * LANES].astype(F32)
@@ -139,6 +152,9 @@
     for d in range(1, n):
         go(meta.at[me], meta.at[me], m_send.at[d], m_recv.at[me], (g, row_peer(d)))
 
+    for c in loads[3:]:
+        c.wait()
+
     r64, c64 = iota((nb, nb), 0), iota((nb, nb), 1)
     dup = onehot(lax.rem(iota((nb, LANES), 1), nb) == iota((nb, LANES), 0))
     lane_b = iota((nb, LANES), 1)
@@ -154,39 +170,54 @@
     spread = jnp.broadcast_to(own_touched, (LANES, LANES)).astype(F32)
     own_kind = jnp.transpose(spread)[0:rows, :]
 
-    def left_tile(t, carry):
-        off = pl.multiple_of(t * LANES, LANES)
-        at = a_ref[0, :, pl.ds(off, LANES)]
-        full = mm(at, w_ref[...])
-        acc = jnp.zeros((rows, LANES), F32)
-        for k in range(kinds):
-            acc = acc + jnp.where(own_kind == k, full[:, k * LANES:(k + 1) * LANES], 0.0)
-        acc = acc.astype(BF16).astype(F32)
-        l3[pl.ds(2 * t, rows, stride=nb), :] = acc
-        l3[pl.ds(2 * t + 1, rows, stride=nb), :] = pltpu.roll(acc, nb, 1)
+    low_half = iota((hrows, LANES), 1) < nb
+    group = 4
+
+    def left_tiles(u, carry):
+        tiles_in = [
+            a_ref[0, :, pl.ds(pl.multiple_of((u * group + v) * LANES, LANES), LANES)]
+            for v in range(group)
+        ]
+        at = jnp.concatenate(tiles_in, axis=0)
+        acc = [jnp.zeros((rows, LANES), F32) for _ in range(group)]
+        for k in range(0, kinds, 2):
+            full = mm(at, w_ref[:, k * LANES:(k + 2) * LANES])
+            for j in range(2):
+                hit = own_kind == k + j
+                for v in range(group):
+                    part = full[v * rows:(v + 1) * rows, j * LANES:(j + 1) * LANES]
+                    acc[v] = jnp.where(hit, part, acc[v])
+        for v in range(group):
+            t = u * group + v
+            val = acc[v].astype(BF16).astype(F32)
+            top, bot = val[0:hrows], val[hrows:rows]
+            even = jnp.where(low_half, top, pltpu.roll(bot, nb, 1))
+            odd = jnp.where(low_half, pltpu.roll(top, nb, 1), bot)
+            l3[pl.ds(2 * t, hrows, stride=nb), :] = even
+            l3[pl.ds(2 * t + 1, hrows, stride=nb), :] = odd
         return carry
 
-    def left_tiles(u, carry):
-        for v in range(4):
-            left_tile(u * 4 + v, carry)
+    lax.fori_loop(0, tiles // group, left_tiles, 0)
+
+    i0, i1 = iota((LANES, LANES), 0), iota((LANES, LANES), 1)
+    same = (i0 < nb) == (i1 < nb)
+    on_diag = lax.rem(iota((nb, LANES), 1), nb) == iota((nb, LANES), 0)
+    unroll = 4
+
+    def product_step(u, carry):
+        for v in range(unroll):
+            i = u * unroll + v
+            off = pl.multiple_of(i * nb, nb)
+            lt = l3[pl.ds(off, nb), :].astype(BF16)
+            zk = jnp.concatenate(
+                [zm_ref[touched_s[0, i]], zm_ref[touched_s[0, i + hrows]]], axis=0
+            )
+            pt = jnp.where(same, mm(zk, lt), 0.0).astype(BF16)
+            ptf = pt[0:nb].astype(F32) + pt[nb:2 * nb].astype(F32)
+            p3[pl.ds(off, nb), :] = jnp.where(on_diag, ptf, ptf + mm_nt(dup, pt))
         return carry
 
-    lax.fori_loop(0, tiles // 4, left_tiles, 0)
-
-    eye = onehot(r64 == c64)
-
-    def product_step(u, carry):
-        for v in range(8):
-            i = u * 8 + v
-            off = pl.multiple_of(i * nb, nb)
-            lt = l3[pl.ds(off, nb), 0:nb].astype(BF16)
-            zk = zm_ref[touched_s[0, i]]
-            pt = mm(zk, lt).astype(BF16)
-            ptf = pt.astype(F32)
-            p3[pl.ds(off, nb), 0:nb] = jnp.where(r64 == c64, ptf, ptf + mm_nt(eye, pt))
-        return carry
-
-    steps = rows // 8
+    steps = hrows // unroll
     if relay:
         lax.fori_loop(0, steps // 2, product_step, 0)
         wait_half(xn, 0)
@@ -203,7 +234,6 @@
     else:
         lax.fori_loop(0, steps, product_step, 0)
 
-    low_lane = lane < nb
     qextra = jnp.zeros((rows, LANES), F32)
 
     def put(t, v):
@@ -212,9 +242,11 @@
         q_ref[rows:2 * rows, t * LANES:(t + 1) * LANES] = lo
 
     def flat_tile(t):
-        even = p3[pl.ds(2 * t, rows, stride=nb), :]
-        odd = p3[pl.ds(2 * t + 1, rows, stride=nb), :]
-        return jnp.where(low_lane, even, pltpu.roll(odd, nb, 1))
+        even = p3[pl.ds(2 * t, hrows, stride=nb), :]
+        odd = p3[pl.ds(2 * t + 1, hrows, stride=nb), :]
+        top = jnp.where(low_half, even, pltpu.roll(odd, nb, 1))
+        bot = jnp.where(low_half, pltpu.roll(even, nb, 1), odd)
+        return jnp.concatenate([top, bot], axis=0)
 
     for t in range(fold):
         top, bottom = flat_tile(t), flat_tile(t + fold)
@@ -286,7 +318,6 @@
         go(zsend.at[d], zrecv.at[g], z_ssem.at[d], z_rsem.at[g], (q, me))
     total = column_slice(g)
 
-    i0, i1 = iota((LANES, LANES), 0), iota((LANES, LANES), 1)
     before = onehot((i0 < i1) & ((i0 < rows) == (i1 < rows)))
     o_id = iota((n, LANES), 0)
     owner = (own_slot >= o_id * rows) & (own_slot < (o_id + 1) * rows)
@@ -323,11 +354,14 @@
     for d in range(1, n):
         s = row_peer(d)
         rdma(osend.at[s], orecv.at[s], o_send.at[d], o_recv.at[s], (g, s)).wait_recv()
-    result = jnp.zeros((rows, cols), F32)
+    high = jnp.zeros((rows, cols), F32)
+    low = jnp.zeros((rows, cols), F32)
     for p in range(pairs):
         hi, lo = split(orecv[2 * p:2 * p + 2].reshape(2 * cap, cols))
-        result = result + mm(lands[p], hi) + mm(lands[p], lo)
-    out_ref[...] = result
+        high = high + mm(lands[p], hi)
+        low = low + mm(lands[p], lo)
+    out_ref[0] = high
+    out_ref[1] = low
     for c in started:
         c.wait_send()
 
@@ -340,20 +374,28 @@
     cap = -(-max(2, rows // n * 2) // 8) * 8
     sends = 14 if n == 8 else 2 * n
     vmem = pl.BlockSpec(memory_space=pltpu.VMEM)
+    hbm = pl.BlockSpec(memory_space=pl.ANY)
     smem = pl.BlockSpec(memory_space=pltpu.SMEM)
     dma = pltpu.SemaphoreType.DMA
-    return pl.pallas_call(
+    parts = pl.pallas_call(
         functools.partial(kernel, n, ng, cap),
-        out_shape=jax.ShapeDtypeStruct((rows, cols), F32),
-        in_specs=[vmem, smem, smem, vmem, vmem, vmem, vmem],
+        out_shape=jax.ShapeDtypeStruct((2, rows, cols), F32),
+        in_specs=[hbm, hbm, smem, hbm, hbm, hbm],
         out_specs=vmem,
         scratch_shapes=[
+            pltpu.VMEM(a_pieces.shape, BF16),
+            pltpu.SMEM(touched.shape, I32),
+            pltpu.VMEM(touched.shape, I32),
+            pltpu.VMEM((1, rows), I32),
+            pltpu.VMEM(x_blocks.shape, BF16),
+            pltpu.VMEM(z_inverse.shape, BF16),
+            dma((6,)),
             pltpu.VMEM((n, rows, packed), BF16),
             pltpu.VMEM((n, 8, LANES), I32),
             pltpu.VMEM((2 * nb, kinds * LANES), BF16),
             pltpu.VMEM((kinds, nb, nb), BF16),
-            pltpu.VMEM((rows * nb, LANES), F32),
-            pltpu.VMEM((rows * nb, LANES), F32),
+            pltpu.VMEM((rows // 2 * nb, LANES), F32),
+            pltpu.VMEM((rows // 2 * nb, LANES), F32),
             pltpu.VMEM((2 * rows, packed), BF16),
             pltpu.VMEM((n // 2, rows, LANES), F32),
             pltpu.VMEM((ng, rows, cols), F32),
@@ -366,7 +408,8 @@
         compiler_params=pltpu.CompilerParams(
             collective_id=0, has_side_effects=True, vmem_limit_bytes=56 * 1024 * 1024
         ),
-    )(a_pieces, touched, block_class, touched, slot_row.reshape(1, rows), x_blocks, z_inverse)
+    )(a_pieces, touched, block_class, slot_row.reshape(1, rows), x_blocks, z_inverse)
+    return parts[0] + parts[1]
 
 
 def solution(mesh):

time: 31.5 us -> 29.3 us (0.930)
  Pallas kernels: 29.9 us -> 27.7 us
  other arithmetic: 0 us -> 1.39 us
  local copies, waits for them, and re-layouts: 1.38 us -> 0 us
    pallas_call x1, Pallas kernels: 29.9 us -> 27.7 us  [shards(): pl.pallas_call(functools.partial(kernel, n, ng, cap), out_shape=jax.Shape...]
    add x0 -> x1, other arithmetic: none -> 1.39 us  [shards(): return parts[0] + parts[1]]
    unnamed x1 -> x0, local copies, waits for them, and re-layouts: 1.38 us -> none
where the time goes in v2:
time: 29.3 us; the launch traced here: 29.1 us
  Pallas kernels  27.7 us (95%)
  other arithmetic  1.39 us (5%)
    pallas_call x1, Pallas kernels, shards(): pl.pallas_call(functools.partial(kernel, n, ng, cap), out_shape=jax.Shape...  27.7 us
    add x1, other arithmetic, shards(): return parts[0] + parts[1]  1.39 us

profile of v2, /device:TPU:0, one launch (start us, length us, event | category | flops | bytes accessed | tf_op | source)
XLA Modules:
  0.0 29.1 jit_solution(5112406746576668679)
XLA Ops:
  0.0 27.7 %shard_map.64 = f32[2,64,128]{2,1,0:T(8,128)} custom-call(bf16[1,64,4096]{2,1,0:T(8,128)(2,1)} %a_hbm.1, s32[1,64]{1,0:T(1,128)} %touched_hbm.1, s32[8]{0:T(128)} %class_s.1, s32[1,64]{1,0:T(1,128)} %bitcast.3, bf16[8,64,64]{2,1,0:T(8,128)(2,1)} %x_hbm.1, bf16[8,64,64]{2,1,0:T(8,128)(2,1)} %z_hbm.1), custom_call_target="tpu_custom_call" | custom-call | tf_op jit(solution)/shard_map/pallas_call | solution.py:380
  27.7 1.4 %add_bitcast_fusion = f32[64,128]{1,0:T(8,128)} fusion(f32[2,64,128]{2,1,0:T(8,128)} %shard_map.64), kind=kLoop, calls=%fused_computation | loop fusion | flops 8192 | bytes 98304 | tf_op jit(solution)/shard_map/add | solution.py:412
